TPU v7x, 32 devices: a whole 2x2x4 slice. The times are simulated.
32 devices in a mesh: site: 2 (over core), rows: 2 (over x), cols: 8 (over z, y).
Axes of the slice: x: 2, y: 2, z: 4, core: 2. Of those that a mesh axis runs over, the one named last changes fastest.
Arguments:
- tracer: float32 [128, 256, 128], P(('site', 'rows'), 'cols'), parts along dimension 0, may hold values from 0.5 to 2
- flow_y: float32 [128, 256, 128], P(('site', 'rows'), 'cols'), parts along dimension 0, may hold values from -0.3 to 0.3
- flow_x: float32 [128, 256, 128], P(('site', 'rows'), 'cols'), parts along dimension 0, may hold values from -0.3 to 0.3
Outputs:
- scaled_field: float32 [128, 256, 128], P(('site', 'rows'), 'cols'), parts along dimension 0
- tracer_end: float32 [128, 256, 128], P(('site', 'rows'), 'cols'), parts along dimension 0
There are 2 independent parts, one for each index of `site`. A program takes and returns all parts, laid end to end along the dimension named above; each array names one. Nothing has to cross between parts.
All inputs are finite; a program needn't handle non-finite values.
Results may differ from a plain program's by a relative error of at most 0.00002.
Values sent between devices are 32-bit elements; how exact they have to be, the bound alone decides.
A program may use at most 64 MiB of HBM per device.

v0:
```python
import functools

import jax
import jax.numpy as jnp
from jax import lax
from jax.experimental import pallas as pl
from jax.experimental.pallas import tpu as pltpu
from jax.sharding import PartitionSpec as P

MESH = pl.DeviceIdType.MESH
DEPTHS = (3, 3)
PAD = 8
SIDES = tuple((dy, dx) for dy in (-1, 0, 1) for dx in (-1, 0, 1) if (dy, dx) != (0, 0))


def spans(side, depth, size, first, low):
    if side == 0:
        return pl.ds(0, size), pl.ds(first, size)
    if side < 0:
        return pl.ds(0, depth), pl.ds(first + size, depth)
    return pl.ds(size - depth, depth), pl.ds(low - depth, depth)


def kernel(rows, cols, by, bx, t_hbm, fy_hbm, fx_hbm, final, moments,
           fields, ping, fy, fx, stats, gathered,
           load_sem, send_sem, recv_sem, stat_send, stat_recv):
    row, col = lax.axis_index("rows"), lax.axis_index("cols")
    top = max(DEPTHS)

    def exists(dy, dx):
        ok = None
        for step, here, count in ((dy, row, rows), (dx, col, cols)):
            if step:
                inside = (here > 0) if step < 0 else (here < count - 1)
                ok = inside if ok is None else jnp.logical_and(ok, inside)
        return ok

    loads = [
        pltpu.make_async_copy(t_hbm, fields.at[0, pl.ds(top, by), pl.ds(0, bx)], load_sem.at[0]),
        pltpu.make_async_copy(fy_hbm, fy.at[pl.ds(top, by), pl.ds(0, bx)], load_sem.at[1]),
        pltpu.make_async_copy(fx_hbm, fx.at[pl.ds(top, by), pl.ds(0, bx)], load_sem.at[2]),
    ]
    for load in loads:
        load.start()

    barrier = pltpu.get_barrier_semaphore()

    @pl.loop(1, cols)
    def _(k):
        pl.semaphore_signal(barrier, inc=1, device_id={"cols": lax.rem(col + k, cols)}, device_id_type=MESH)

    for dy, dx in SIDES:
        if dy:
            @pl.when(exists(dy, dx))
            def _():
                pl.semaphore_signal(barrier, inc=1, device_id={"rows": row + dy, "cols": col + dx},
                                    device_id_type=MESH)

    width = bx + PAD
    for dy in (-1, 1):
        lines = pl.ds(0, top) if dy < 0 else pl.ds(top + by, top)

        @pl.when(jnp.logical_not(exists(dy, 0)))
        def _():
            blank = jnp.zeros((top, width, 128), jnp.float32)
            for e in range(len(DEPTHS)):
                fields[e, lines] = blank
            for b in range(2):
                ping[b, lines] = blank
            fy[lines] = blank
            fx[lines] = blank
    for dx in (-1, 1):
        strip = pl.ds(width - PAD // 2, PAD // 2) if dx < 0 else pl.ds(bx, PAD // 2)

        @pl.when(jnp.logical_not(exists(0, dx)))
        def _():
            @pl.loop(0, by + 2 * top)
            def _(y):
                blank = jnp.zeros((PAD // 2, 128), jnp.float32)
                for e in range(len(DEPTHS)):
                    fields[e, y, strip] = blank
                fy[y, strip] = blank
                fx[y, strip] = blank

    def one(n, count):
        return (n + count - 1) // count

    upright = one(row, rows) + one(rows - 1 - row, rows)
    across = one(col, cols) + one(cols - 1 - col, cols)
    pl.semaphore_wait(barrier, cols - 1 + upright * (1 + across))

    def copies(e, side):
        dy, dx = SIDES[side]
        target = {"rows": row + dy, "cols": col + dx}
        corner = 1 if dy and dx else 0
        out = []
        depth = DEPTHS[e]
        jobs = [(t_hbm if e == 0 else None, fields.at[e], depth - corner)]
        if e == 0:
            jobs += [(fy_hbm, fy, top - 1 - corner), (fx_hbm, fx, top - 1 - corner)]
        for i, (src, dst, d) in enumerate(jobs):
            if d <= 0:
                continue
            ys, yd = spans(dy, d, by, top, top)
            xs, xd = spans(dx, d, bx, 0, width)
            if src is None:
                src = fields.at[e, pl.ds(top, by), pl.ds(0, bx)]
            out.append(pltpu.make_async_remote_copy(
                src_ref=src.at[ys, xs], dst_ref=dst.at[yd, xd],
                send_sem=send_sem.at[e, side, i], recv_sem=recv_sem.at[e, side, i],
                device_id=target, device_id_type=MESH))
        return out

    def start(e):
        for i in range(3):
            for side, (dy, dx) in enumerate(SIDES):
                mine = copies(e, side)
                if i < len(mine):
                    @pl.when(exists(dy, dx))
                    def _():
                        mine[i].start()

    def finish(e):
        for side, (dy, dx) in enumerate(SIDES):
            @pl.when(exists(-dy, -dx))
            def _():
                for copy in copies(e, side):
                    copy.wait_recv()

    def drain(e):
        for side, (dy, dx) in enumerate(SIDES):
            @pl.when(exists(dy, dx))
            def _():
                for copy in copies(e, side):
                    copy.wait_send()

    column = lax.broadcasted_iota(jnp.int32, (1, width, 128), 1)
    keep = jnp.logical_and(
        jnp.logical_or(column < bx + PAD // 2, jnp.broadcast_to(col > 0, column.shape)),
        jnp.logical_or(jnp.logical_or(column < bx, column >= bx + PAD // 2),
                       jnp.broadcast_to(col < cols - 1, column.shape)))

    def update(src, y, k):
        c = src[pl.ds(y, k)]
        above, below = src[pl.ds(y + 1, k)], src[pl.ds(y - 1, k)]
        right, left = pltpu.roll(c, width - 1, 1), pltpu.roll(c, 1, 1)
        spread = (above + below) + (right + left)
        return (0.8 * c + 0.05 * spread) - fy[pl.ds(y, k)] * (above - below) - fx[pl.ds(y, k)] * (right - left)

    def advance(src, dst, margin):
        k = 8

        @pl.loop(0, by // k)
        def _(i):
            y = top + i * k
            dst[pl.ds(y, k)] = jnp.where(keep, update(src, y, k), 0.0)
        for dy in (-1, 1):
            @pl.when(exists(dy, 0))
            def _():
                y = top - margin if dy < 0 else top + by
                for j in range(margin):
                    dst[pl.ds(y + j, 1)] = jnp.where(keep, update(src, y + j, 1), 0.0)

    def advance_last(src, write):
        k = 8

        @pl.loop(0, by // k)
        def _(i):
            y = top + i * k
            write(i * k, k, update(src, y, k)[:, :bx])

    start(0)
    for load in loads:
        load.wait()
    for e, depth in enumerate(DEPTHS):
        finish(e)
        src = fields.at[e]
        for s in range(depth - 1):
            dst = ping.at[s % 2]
            advance(src, dst, depth - 1 - s)
            src = dst
        if e + 1 < len(DEPTHS):
            def write(y, k, new):
                fields[e + 1, pl.ds(top + y, k), pl.ds(0, bx)] = new
            advance_last(src, write)
            start(e + 1)
        else:
            def write(y, k, new):
                final[pl.ds(y, k)] = new
            advance_last(src, write)

    g = 8

    @pl.loop(0, by // g)
    def _(i):
        block = final[pl.ds(i * g, g)]
        mean = jnp.sum(block, axis=1) / bx
        off = block - mean[:, None, :]
        stats[0, pl.ds(i * g, g)] = mean
        stats[1, pl.ds(i * g, g)] = jnp.sum(off * off, axis=1)

    def share(k):
        return pltpu.make_async_remote_copy(
            src_ref=stats, dst_ref=gathered.at[k - 1],
            send_sem=stat_send.at[k - 1], recv_sem=stat_recv.at[k - 1],
            device_id={"cols": lax.rem(col + k, cols)}, device_id_type=MESH)

    @pl.loop(1, cols)
    def _(k):
        share(k).start()

    @pl.loop(1, cols)
    def _(k):
        share(k).wait_recv()

    @pl.loop(0, by // g)
    def _(i):
        lines = pl.ds(i * g, g)
        mean0 = stats[0, lines]
        mean = (mean0 + jnp.sum(gathered[:, 0, lines], axis=0)) / cols
        d0 = mean0 - mean
        d = gathered[:, 0, lines] - mean
        spread = stats[1, lines] + bx * (d0 * d0) + jnp.sum(gathered[:, 1, lines] + bx * (d * d), axis=0)
        moments[0, lines] = mean
        moments[1, lines] = lax.rsqrt(spread / (bx * cols) + 0.0001)
    for e in range(len(DEPTHS)):
        drain(e)

    @pl.loop(1, cols)
    def _(k):
        share(k).wait_send()


def scale_kernel(end, lines, scaled_out, end_out, scaled, sem):
    parts = 4
    g = end.shape[0] // parts
    whole = pltpu.make_async_copy(end, end_out, sem.at[parts])
    stores = [whole]
    for i in range(parts):
        part = pl.ds(i * g, g)
        scaled[part] = (end[part] - lines[0, part][:, None, :]) * lines[1, part][:, None, :]
        store = pltpu.make_async_copy(scaled.at[part], scaled_out.at[part], sem.at[i])
        store.start()
        stores.append(store)
        if i == 0:
            whole.start()
    for store in stores:
        store.wait()


def shards(rows, cols, tracer, flow_y, flow_x):
    by, bx, species = tracer.shape
    top = max(DEPTHS)
    exchanges = len(DEPTHS)
    padded = (by + 2 * top, bx + PAD, species)
    block = jax.ShapeDtypeStruct(tracer.shape, jnp.float32)
    hbm = pl.BlockSpec(memory_space=pl.ANY)
    end, lines = pl.pallas_call(
        functools.partial(kernel, rows, cols, by, bx),
        out_shape=(pltpu.VMEM(tracer.shape, jnp.float32), pltpu.VMEM((2, by, species), jnp.float32)),
        in_specs=[pl.BlockSpec(memory_space=pltpu.HBM)] * 3,
        out_specs=(pl.BlockSpec(memory_space=pltpu.VMEM),) * 2,
        scratch_shapes=[
            pltpu.VMEM((exchanges,) + padded, jnp.float32),
            pltpu.VMEM((2,) + padded, jnp.float32),
            pltpu.VMEM(padded, jnp.float32),
            pltpu.VMEM(padded, jnp.float32),
            pltpu.VMEM((2, by, species), jnp.float32),
            pltpu.VMEM((cols - 1, 2, by, species), jnp.float32),
            pltpu.SemaphoreType.DMA((3,)),
            pltpu.SemaphoreType.DMA((exchanges, 8, 3)),
            pltpu.SemaphoreType.DMA((exchanges, 8, 3)),
            pltpu.SemaphoreType.DMA((cols - 1,)),
            pltpu.SemaphoreType.DMA((cols - 1,)),
        ],
        compiler_params=pltpu.CompilerParams(
            collective_id=0, has_side_effects=True, vmem_limit_bytes=67043328 - 1024 * 1024),
    )(tracer, flow_y, flow_x)
    return pl.pallas_call(
        scale_kernel,
        out_shape=(block, block),
        in_specs=[pl.BlockSpec(memory_space=pltpu.VMEM)] * 2,
        out_specs=(hbm, hbm),
        scratch_shapes=[
            pltpu.VMEM(tracer.shape, jnp.float32),
            pltpu.SemaphoreType.DMA((5,)),
        ],
        compiler_params=pltpu.CompilerParams(vmem_limit_bytes=40 * 1024 * 1024),
    )(end, lines)


def solution(mesh):
    placed = P(("site", "rows"), "cols", None)
    return jax.shard_map(
        functools.partial(shards, mesh.shape["rows"], mesh.shape["cols"]),
        mesh=mesh,
        in_specs=(placed,) * 3,
        out_specs=(placed, placed),
        check_vma=False,
    )
```

profile of v0, /device:TPU:0, one launch (start us, length us, event | category | flops | bytes accessed | tf_op | source)
XLA Modules:
  0.0 26.8 jit_solution(2355714694622571506)
XLA Ops:
  0.6 25.1 %shard_map.50 = (f32[32,32,128]{2,1,0:T(8,128)S(1)}, f32[2,32,128]{2,1,0:T(8,128)S(1)}) custom-call(f32[32,32,128]{2,1,0:T(8,128)} %t_hbm.1, f32[32,32,128]{2,1,0:T(8,128)} %fy_hbm.1, f32[32,32,128]{2,1,0:T(8,128)} %fx_hbm.1), custom_call_target="tpu_custom_call" | custom-call | tf_op jit(solution)/shard_map/pallas_call | solution.py:258
  25.8 1.0 %shard_map.51 = (f32[32,32,128]{2,1,0:T(8,128)}, f32[32,32,128]{2,1,0:T(8,128)}) custom-call(f32[32,32,128]{2,1,0:T(8,128)S(1)} %get-tuple-element.4.end, f32[2,32,128]{2,1,0:T(8,128)S(1)} %get-tuple-element.5.lines), custom_call_target="tpu_custom_call" | custom-call | tf_op jit(solution)/shard_map/pallas_call | solution.py:279
where the time goes:
time: 26.9 us; the launch traced here: 26.8 us
  Pallas kernels  26.1 us (97%)
  between operations  0.64 us (2%)
    pallas_call x1, Pallas kernels, shards(): pl.pallas_call(functools.partial(kernel, rows, cols, by, bx), out_shape=(...  25.1 us
    pallas_call x1, Pallas kernels, shards(): pl.pallas_call(scale_kernel, out_shape=(block, block), in_specs=[pl.Block...  1.02 us

commit v1 on v0

v1 whole, which is shorter than its diff:
```python
import functools

import jax
import jax.numpy as jnp
from jax import lax
from jax.experimental import pallas as pl
from jax.experimental.pallas import tpu as pltpu
from jax.sharding import PartitionSpec as P

MESH = pl.DeviceIdType.MESH
STEPS, DEPTH = 6, 3
PHASES = STEPS // DEPTH
PAD = 8
HALF = PAD // 2
CUTS = (8,)
SIDES = tuple((dy, dx) for dy in (-1, 1, 0) for dx in (-1, 1, 0) if (dy, dx) != (0, 0))
CORNERS = tuple(side for side in SIDES if side[0] and side[1])


def radii(cols):
    out, r = [], 1
    while r < cols - 1:
        out.append(r)
        r *= 2
    return out


def kernel(rows, cols, by, bx, cuts, t_hbm, fy_hbm, fx_hbm, final, moments,
           main, halo, f, fh, weight, stats, gathered,
           load_sem, col_send, col_recv, row_send, row_recv, corner_send, corner_recv,
           stat_send, stat_recv, tokens):
    row, col = lax.axis_index("rows"), lax.axis_index("cols")
    top = DEPTH
    tall = by + 2 * top
    chunks = len(cuts) - 1
    odd = lax.rem(row, 2) == 1

    def exists(dy, dx):
        ok = None
        for step, here, count in ((dy, row, rows), (dx, col, cols)):
            if step:
                inside = (here > 0) if step < 0 else (here < count - 1)
                ok = inside if ok is None else jnp.logical_and(ok, inside)
        return ok

    def at(v, n):
        return jnp.where(odd, top + v, top + by - v - n)

    barrier = pltpu.get_barrier_semaphore()
    for dy, dx in SIDES:
        if dy and dx:
            continue

        @pl.when(exists(dy, dx))
        def _():
            pl.semaphore_signal(barrier, inc=1, device_id={"rows": row + dy, "cols": col + dx},
                                device_id_type=MESH)

    loads = [
        pltpu.make_async_copy(t_hbm, main.at[0, pl.ds(top, by)], load_sem.at[0]),
        pltpu.make_async_copy(fy_hbm, f.at[0, pl.ds(top, by)], load_sem.at[1]),
        pltpu.make_async_copy(fx_hbm, f.at[1, pl.ds(top, by)], load_sem.at[2]),
    ]
    for load in loads:
        load.start()

    for dy in (-1, 1):
        line = top - 1 if dy < 0 else top + by

        @pl.when(jnp.logical_not(exists(dy, 0)))
        def _():
            for s in range(STEPS):
                main[s, line] = jnp.zeros((bx, 128), jnp.float32)
                halo[s, line] = jnp.zeros((PAD, 128), jnp.float32)
    for dx in (-1, 1):
        strip = pl.ds(HALF, HALF) if dx < 0 else pl.ds(0, HALF)

        @pl.when(jnp.logical_not(exists(0, dx)))
        def _():
            for p in range(PHASES):
                halo[p * DEPTH, :, strip] = jnp.zeros((tall, HALF, 128), jnp.float32)

    def one(n, count):
        return (n + count - 1) // count

    def on_both(r):
        return jnp.where(col >= r, 1, 0) + jnp.where(col < cols - r, 1, 0)

    upright = one(row, rows) + one(rows - 1 - row, rows)
    across = on_both(1)

    for load in loads:
        load.wait()

    @pl.loop(0, by // 4)
    def _(i):
        lines = pl.ds(i * 4, 4)
        for d in range(2):
            flow = f[d, pl.ds(top + i * 4, 4)]
            weight[2 * d, lines] = 0.05 - flow
            weight[2 * d + 1, lines] = 0.05 + flow
    pl.semaphore_wait(barrier, across + upright)

    spread_to = radii(cols)

    def send_token(i):
        if i < len(spread_to):
            r = spread_to[i]
            for sign in (-1, 1):
                @pl.when((col >= r) if sign < 0 else (col < cols - r))
                def _():
                    pl.semaphore_signal(tokens.at[i], inc=1, device_id={"cols": col + sign * r},
                                        device_id_type=MESH)

    def take_token(i):
        if i < len(spread_to):
            pl.semaphore_wait(tokens.at[i], on_both(spread_to[i]))

    def remote(src, dst, send, recv, dy, dx):
        return pltpu.make_async_remote_copy(
            src_ref=src, dst_ref=dst, send_sem=send, recv_sem=recv,
            device_id={"rows": row + dy, "cols": col + dx}, device_id_type=MESH)

    def cols_of(dx, depth):
        if dx > 0:
            return pl.ds(bx - depth, depth), pl.ds(PAD - depth, depth)
        return pl.ds(0, depth), pl.ds(0, depth)

    def rows_of(dy, depth):
        if dy > 0:
            return pl.ds(top + by - depth, depth), pl.ds(top - depth, depth)
        return pl.ds(top, depth), pl.ds(top + by, depth)

    def reach(p, c):
        if c < 0:
            return 0
        return by if c == chunks - 1 else min(by, cuts[c + 1] + STEPS - 1 - p * DEPTH)

    def column_copies(p, c):
        v, n = reach(p, c - 1), reach(p, c) - reach(p, c - 1)
        out = []
        if not n:
            return out
        lines = pl.ds(at(v, n), n)
        for i, dx in enumerate((-1, 1)):
            xs, xd = cols_of(dx, DEPTH)
            mine = [remote(main.at[p * DEPTH, lines, xs], halo.at[p * DEPTH, lines, xd],
                           col_send.at[p, c, i, 0], col_recv.at[p, c, i, 0], 0, dx)]
            if p == 0:
                xs, xd = cols_of(dx, DEPTH - 1)
                mine.append(remote(f.at[:, lines, xs], fh.at[:, lines, xd],
                                   col_send.at[p, c, i, 1], col_recv.at[p, c, i, 1], 0, dx))
            out.append((exists(0, dx), exists(0, -dx), mine))
        return out

    def border_copies(p, first, corners):
        out = []
        for i, dy in enumerate((-1, 1)):
            here = odd if (dy < 0) == first else jnp.logical_not(odd)
            there = odd if (dy > 0) == first else jnp.logical_not(odd)
            ys, yd = rows_of(dy, DEPTH)
            mine = [remote(main.at[p * DEPTH, ys], main.at[p * DEPTH, yd],
                           row_send.at[p, i, 0], row_recv.at[p, i, 0], dy, 0)]
            if p == 0:
                ys, yd = rows_of(dy, DEPTH - 1)
                mine.append(remote(f.at[:, ys], f.at[:, yd],
                                   row_send.at[p, i, 1], row_recv.at[p, i, 1], dy, 0))
            if not corners:
                out.append((jnp.logical_and(here, exists(dy, 0)), jnp.logical_and(there, exists(-dy, 0)), mine))
                continue
            for j, dx in enumerate((-1, 1)):
                (ys, yd), (xs, xd) = rows_of(dy, DEPTH - 1), cols_of(dx, DEPTH - 1)
                mine = [remote(main.at[p * DEPTH, ys, xs], halo.at[p * DEPTH, yd, xd],
                               corner_send.at[p, i, j, 0], corner_recv.at[p, i, j, 0], dy, dx)]
                if p == 0 and DEPTH > 2:
                    (ys, yd), (xs, xd) = rows_of(dy, DEPTH - 2), cols_of(dx, DEPTH - 2)
                    mine.append(remote(f.at[:, ys, xs], fh.at[:, yd, xd],
                                       corner_send.at[p, i, j, 1], corner_recv.at[p, i, j, 1], dy, dx))
                out.append((jnp.logical_and(here, exists(dy, dx)),
                            jnp.logical_and(there, exists(-dy, -dx)), mine))
        return out

    def corner_copies(p, c):
        out = []
        if c == 0:
            out = border_copies(p, True, True)
        if c == chunks - 1 and rows > 2:
            out = out + border_copies(p, False, True)
        return out

    def side_copies(p, c):
        out = column_copies(p, c)
        if c == 0:
            out = out + border_copies(p, True, False)
        if c == chunks - 1 and rows > 2:
            out = out + border_copies(p, False, False)
        return out

    def exchange(p, c):
        return corner_copies(p, c) + side_copies(p, c)

    def start(jobs):
        for here, _, copies in jobs:
            @pl.when(here)
            def _():
                for copy in copies:
                    copy.start()

    def finish(jobs):
        for _, there, copies in jobs:
            @pl.when(there)
            def _():
                for copy in copies:
                    copy.wait_recv()

    def drain(jobs):
        for here, _, copies in jobs:
            @pl.when(here)
            def _():
                for copy in copies:
                    copy.wait_send()

    column = lax.broadcasted_iota(jnp.int32, (1, PAD, 128), 1)
    keep = jnp.logical_and(
        jnp.logical_or(column < HALF, jnp.broadcast_to(col > 0, column.shape)),
        jnp.logical_or(column >= HALF, jnp.broadcast_to(col < cols - 1, column.shape)))

    def mix(c, above, below, right, left, fy, fx):
        spread = (above + below) + (right + left)
        return (0.8 * c + 0.05 * spread) - fy * (above - below) - fx * (right - left)

    def new_main(s, y, k, beyond=False):
        c = main[s, pl.ds(y, k)]
        wide = jnp.concatenate([c, halo[s, pl.ds(y, k)]], axis=1)
        right, left = pltpu.roll(wide, bx + PAD - 1, 1)[:, :bx], pltpu.roll(wide, 1, 1)[:, :bx]
        above, below = main[s, pl.ds(y + 1, k)], main[s, pl.ds(y - 1, k)]
        if beyond:
            return mix(c, above, below, right, left, f[0, pl.ds(y, k)], f[1, pl.ds(y, k)])
        up, down, ahead, back = (weight[i, pl.ds(y - top, k)] for i in range(4))
        return ((0.8 * c + up * above) + down * below) + (ahead * right + back * left)

    def new_halo(s, y, k):
        c = halo[s, pl.ds(y, k)]
        wide = jnp.concatenate([main[s, pl.ds(y, k), pl.ds(bx - PAD, PAD)], c,
                                main[s, pl.ds(y, k), pl.ds(0, PAD)]], axis=1)
        right = pltpu.roll(wide, 3 * PAD - 1, 1)[:, PAD:2 * PAD]
        left = pltpu.roll(wide, 1, 1)[:, PAD:2 * PAD]
        new = mix(c, halo[s, pl.ds(y + 1, k)], halo[s, pl.ds(y - 1, k)], right, left,
                  fh[0, pl.ds(y, k)], fh[1, pl.ds(y, k)])
        return jnp.where(keep, new, 0.0)

    def over(v, n, k, do):
        if n <= 0:
            return
        y = at(v, n)
        whole = n // k
        if whole > 1:
            @pl.loop(0, whole)
            def _(i):
                do(y + i * k, k)
        elif whole:
            do(y, k)
        if n % k:
            do(y + whole * k, n % k)

    def write_main(s, beyond=False):
        def do(y, k):
            main[s, pl.ds(y, k)] = new_main(s - 1, y, k, beyond)
        return do

    def write_halo(s):
        def do(y, k):
            halo[s, pl.ds(y, k)] = new_halo(s - 1, y, k)
        return do

    def advance(p, c):
        for i in range(1, DEPTH + 1):
            s = p * DEPTH + i
            ahead = STEPS - s
            low = 0 if c == 0 else min(by, cuts[c] + ahead)
            high = by if c == chunks - 1 else min(by, cuts[c + 1] + ahead)
            if s == STEPS:
                break
            over(low, high - low, 8, write_main(s))
            if i < DEPTH:
                low = low - 1 if c else 0
                high = high if c == chunks - 1 else high - 1
                over(low, high - low, 16, write_halo(s))
                margin = DEPTH - i
                for first in (True, False):
                    if c != (0 if first else chunks - 1) or not first and rows <= 2:
                        continue
                    for dy in (-1, 1):
                        here = odd if (dy < 0) == first else jnp.logical_not(odd)

                        @pl.when(jnp.logical_and(here, exists(dy, 0)))
                        def _():
                            y = top - margin if dy < 0 else top + by
                            write_main(s, True)(y, margin)
                            write_halo(s)(y, margin)
        return low, high

    def share(c, to, sender):
        n = cuts[c + 1] - cuts[c]
        lines = pl.ds(pl.multiple_of(at(cuts[c], n) - top, 8), n)
        return pltpu.make_async_remote_copy(
            src_ref=stats.at[:, lines], dst_ref=gathered.at[sender, :, lines],
            send_sem=stat_send.at[c, to], recv_sem=stat_recv.at[c, sender],
            device_id={"cols": to}, device_id_type=MESH)

    def each_peer(do):
        if cols <= 8:
            for k in range(cols):
                @pl.when(col != k)
                def _():
                    do(k)
        else:
            @pl.loop(0, cols)
            def _(k):
                @pl.when(col != k)
                def _():
                    do(k)

    def last_step(v, n):
        y = at(v, n)

        @pl.loop(0, n // 8)
        def _(i):
            new = new_main(STEPS - 1, y + i * 8, 8)
            out = pl.ds(pl.multiple_of(y - top + i * 8, 8), 8)
            final[out] = new
            mean = jnp.sum(new, axis=1) / bx
            off = new - mean[:, None, :]
            second = jnp.sum(off * off, axis=1)
            stats[0, out] = mean
            stats[1, out] = second
            gathered[col, 0, out] = mean
            gathered[col, 1, out] = second

    def combine(c):
        n = cuts[c + 1] - cuts[c]
        y = at(cuts[c], n) - top

        @pl.loop(0, n // 8)
        def _(i):
            lines = pl.ds(pl.multiple_of(y + i * 8, 8), 8)
            means = [gathered[k, 0, lines] for k in range(cols)]
            mean = sum(means[1:], means[0]) / cols
            parts = [gathered[k, 1, lines] + bx * ((means[k] - mean) * (means[k] - mean)) for k in range(cols)]
            spread = sum(parts[1:], parts[0])
            moments[0, lines] = mean
            moments[1, lines] = lax.rsqrt(spread / (bx * cols) + 0.0001)

    send_token(0)
    for c in range(chunks):
        start(side_copies(0, c))
    known = 0

    def learn():
        take_token(known)
        send_token(known + 1)
        return known + 1

    if spread_to:
        known = learn()
    for c in range(chunks):
        start(corner_copies(0, c))
    while known < len(spread_to) - 1:
        known = learn()
    for p in range(PHASES):
        for c in range(chunks):
            finish(exchange(p, c))
            low, high = advance(p, c)
            if p + 1 < PHASES:
                start(exchange(p + 1, c))
            else:
                last_step(low, high - low)
                while known < len(spread_to):
                    known = learn()
                each_peer(lambda k: share(c, k, col).start())
    for c in range(chunks):
        each_peer(lambda k: share(c, k, k).wait_recv())
        combine(c)
    for c in range(chunks):
        for p in range(PHASES):
            drain(exchange(p, c))
        each_peer(lambda k: share(c, k, col).wait_send())


def scale_kernel(end, lines, scaled_out, end_out, scaled, sem):
    parts = 4
    g = end.shape[0] // parts
    whole = pltpu.make_async_copy(end, end_out, sem.at[parts])
    stores = [whole]
    for i in range(parts):
        part = pl.ds(i * g, g)
        scaled[part] = (end[part] - lines[0, part][:, None, :]) * lines[1, part][:, None, :]
        store = pltpu.make_async_copy(scaled.at[part], scaled_out.at[part], sem.at[i])
        store.start()
        stores.append(store)
        if i == 0:
            whole.start()
    for store in stores:
        store.wait()


def shards(rows, cols, tracer, flow_y, flow_x):
    by, bx, species = tracer.shape
    cuts = (0,) + tuple(cut for cut in CUTS if cut < by) + (by,)
    chunks = len(cuts) - 1
    tall = by + 2 * DEPTH
    block = jax.ShapeDtypeStruct(tracer.shape, jnp.float32)
    hbm = pl.BlockSpec(memory_space=pl.ANY)
    dma = pltpu.SemaphoreType.DMA
    end, lines = pl.pallas_call(
        functools.partial(kernel, rows, cols, by, bx, cuts),
        out_shape=(pltpu.VMEM(tracer.shape, jnp.float32), pltpu.VMEM((2, by, species), jnp.float32)),
        in_specs=[pl.BlockSpec(memory_space=pltpu.HBM)] * 3,
        out_specs=(pl.BlockSpec(memory_space=pltpu.VMEM),) * 2,
        scratch_shapes=[
            pltpu.VMEM((STEPS, tall, bx, species), jnp.float32),
            pltpu.VMEM((STEPS, tall, PAD, species), jnp.float32),
            pltpu.VMEM((2, tall, bx, species), jnp.float32),
            pltpu.VMEM((2, tall, PAD, species), jnp.float32),
            pltpu.VMEM((4, by, bx, species), jnp.float32),
            pltpu.VMEM((2, by, species), jnp.float32),
            pltpu.VMEM((cols, 2, by, species), jnp.float32),
            dma((3,)),
            dma((PHASES, chunks, 2, 2)), dma((PHASES, chunks, 2, 2)),
            dma((PHASES, 2, 2)), dma((PHASES, 2, 2)),
            dma((PHASES, 2, 2, 2)), dma((PHASES, 2, 2, 2)),
            dma((chunks, cols)), dma((chunks, cols)),
            pltpu.SemaphoreType.REGULAR((max(1, len(radii(cols))),)),
        ],
        compiler_params=pltpu.CompilerParams(
            collective_id=0, has_side_effects=True, vmem_limit_bytes=67043328 - 1024 * 1024),
    )(tracer, flow_y, flow_x)
    return pl.pallas_call(
        scale_kernel,
        out_shape=(block, block),
        in_specs=[pl.BlockSpec(memory_space=pltpu.VMEM)] * 2,
        out_specs=(hbm, hbm),
        scratch_shapes=[
            pltpu.VMEM(tracer.shape, jnp.float32),
            pltpu.SemaphoreType.DMA((5,)),
        ],
        compiler_params=pltpu.CompilerParams(vmem_limit_bytes=40 * 1024 * 1024),
    )(end, lines)


def solution(mesh):
    placed = P(("site", "rows"), "cols", None)
    return jax.shard_map(
        functools.partial(shards, mesh.shape["rows"], mesh.shape["cols"]),
        mesh=mesh,
        in_specs=(placed,) * 3,
        out_specs=(placed, placed),
        check_vma=False,
    )
```

time: 26.9 us -> 25.6 us (0.952)
  Pallas kernels: 26.1 us -> 24.8 us
    pallas_call x1, Pallas kernels: 25.1 us -> 23.8 us  [shards(): pl.pallas_call(functools.partial(kernel, rows, cols, by, bx, cuts), out_s...]
where the time goes in v1:
time: 25.6 us; the launch traced here: 25.5 us
  Pallas kernels  24.8 us (97%)
  between operations  0.64 us (2%)
    pallas_call x1, Pallas kernels, shards(): pl.pallas_call(functools.partial(kernel, rows, cols, by, bx, cuts), out_s...  23.8 us
    pallas_call x1, Pallas kernels, shards(): pl.pallas_call(scale_kernel, out_shape=(block, block), in_specs=[pl.Block...  1.02 us

profile of v1, /device:TPU:0, one launch (start us, length us, event | category | flops | bytes accessed | tf_op | source)
XLA Modules:
  0.0 25.5 jit_solution(11715252079657971937)
XLA Ops:
  0.6 23.8 %shard_map.50 = (f32[32,32,128]{2,1,0:T(8,128)S(1)}, f32[2,32,128]{2,1,0:T(8,128)S(1)}) custom-call(f32[32,32,128]{2,1,0:T(8,128)} %t_hbm.1, f32[32,32,128]{2,1,0:T(8,128)} %fy_hbm.1, f32[32,32,128]{2,1,0:T(8,128)} %fx_hbm.1), custom_call_target="tpu_custom_call" | custom-call | tf_op jit(solution)/shard_map/pallas_call | solution.py:415
  24.4 1.0 %shard_map.51 = (f32[32,32,128]{2,1,0:T(8,128)}, f32[32,32,128]{2,1,0:T(8,128)}) custom-call(f32[32,32,128]{2,1,0:T(8,128)S(1)} %get-tuple-element.4.end, f32[2,32,128]{2,1,0:T(8,128)S(1)} %get-tuple-element.5.lines), custom_call_target="tpu_custom_call" | custom-call | tf_op jit(solution)/shard_map/pallas_call | solution.py:438

commit v2 on v1

--- a/solution.py
+++ b/solution.py
@@ -13,6 +13,9 @@
 PAD = 8
 HALF = PAD // 2
 CUTS = (8,)
+FINE = (8,)
+HEAD = 2
+HOLD = 1600
 SIDES = tuple((dy, dx) for dy in (-1, 1, 0) for dx in (-1, 1, 0) if (dy, dx) != (0, 0))
 CORNERS = tuple(side for side in SIDES if side[0] and side[1])
 
@@ -25,14 +28,15 @@
     return out
 
 
-def kernel(rows, cols, by, bx, cuts, t_hbm, fy_hbm, fx_hbm, final, moments,
-           main, halo, f, fh, weight, stats, gathered,
+def kernel(rows, cols, by, bx, cuts, fine, t_hbm, fy_hbm, fx_hbm, final, moments,
+           main, halo, f, fh, weight, early, landed, stats, gathered,
            load_sem, col_send, col_recv, row_send, row_recv, corner_send, corner_recv,
-           stat_send, stat_recv, tokens):
+           edge_send, edge_recv,           stat_send, stat_recv, tokens):
     row, col = lax.axis_index("rows"), lax.axis_index("cols")
     top = DEPTH
     tall = by + 2 * top
     chunks = len(cuts) - 1
+    plan = [cuts] * (PHASES - 1) + [fine]
     odd = lax.rem(row, 2) == 1
 
     def exists(dy, dx):
@@ -88,18 +92,6 @@
 
     upright = one(row, rows) + one(rows - 1 - row, rows)
     across = on_both(1)
-
-    for load in loads:
-        load.wait()
-
-    @pl.loop(0, by // 4)
-    def _(i):
-        lines = pl.ds(i * 4, 4)
-        for d in range(2):
-            flow = f[d, pl.ds(top + i * 4, 4)]
-            weight[2 * d, lines] = 0.05 - flow
-            weight[2 * d + 1, lines] = 0.05 + flow
-    pl.semaphore_wait(barrier, across + upright)
 
     spread_to = radii(cols)
 
@@ -136,6 +128,9 @@
             return 0
         return by if c == chunks - 1 else min(by, cuts[c + 1] + STEPS - 1 - p * DEPTH)
 
+    def near_side(first):
+        return jnp.where(odd, row > 0, row < rows - 1) if first else jnp.where(odd, row < rows - 1, row > 0)
+
     def column_copies(p, c):
         v, n = reach(p, c - 1), reach(p, c) - reach(p, c - 1)
         out = []
@@ -143,14 +138,42 @@
             return out
         lines = pl.ds(at(v, n), n)
         for i, dx in enumerate((-1, 1)):
-            xs, xd = cols_of(dx, DEPTH)
+            xs, xd = cols_of(dx, DEPTH - 1)
             mine = [remote(main.at[p * DEPTH, lines, xs], halo.at[p * DEPTH, lines, xd],
                            col_send.at[p, c, i, 0], col_recv.at[p, c, i, 0], 0, dx)]
             if p == 0:
-                xs, xd = cols_of(dx, DEPTH - 1)
+                xs, xd = cols_of(dx, 1)
                 mine.append(remote(f.at[:, lines, xs], fh.at[:, lines, xd],
                                    col_send.at[p, c, i, 1], col_recv.at[p, c, i, 1], 0, dx))
             out.append((exists(0, dx), exists(0, -dx), mine))
+        return out
+
+    def ahead_copies(p, c):
+        v, n = reach(p, c - 1), reach(p, c) - reach(p, c - 1)
+        if not n:
+            return []
+        lines = pl.ds(at(v, n), n)
+        out = []
+        for i, dx in enumerate((-1, 1)):
+            x = pl.ds(1, 1) if dx < 0 else pl.ds(PAD - 2, 1)
+            out.append((exists(0, dx), exists(0, -dx), [
+                remote(early.at[p, i, lines, x], landed.at[p, lines, x],
+                       col_send.at[p, c, i, 2], col_recv.at[p, c, i, 2], 0, dx)]))
+        return out
+
+    def edge_copies(p, first):
+        e, out = 0 if first else 1, []
+        y = pl.ds(at(0 if first else by - 1, 1), 1)
+        for i, dx in enumerate((-1, 1)):
+            xs, xd = (pl.ds(2, 1),) * 2 if dx < 0 else (pl.ds(bx - 3, 1), pl.ds(PAD - 3, 1))
+            mine = [remote(main.at[p * DEPTH, y, xs], halo.at[p * DEPTH, y, xd],
+                           edge_send.at[p, e, i, 0], edge_recv.at[p, e, i, 0], 0, dx)]
+            if p == 0:
+                xs, xd = (pl.ds(1, 1),) * 2 if dx < 0 else (pl.ds(bx - 2, 1), pl.ds(PAD - 2, 1))
+                mine.append(remote(f.at[:, y, xs], fh.at[:, y, xd],
+                                   edge_send.at[p, e, i, 1], edge_recv.at[p, e, i, 1], 0, dx))
+            out.append((jnp.logical_and(near_side(first), exists(0, dx)),
+                        jnp.logical_and(near_side(first), exists(0, -dx)), mine))
         return out
 
     def border_copies(p, first, corners):
@@ -183,9 +206,9 @@
     def corner_copies(p, c):
         out = []
         if c == 0:
-            out = border_copies(p, True, True)
+            out = border_copies(p, True, True) + edge_copies(p, True)
         if c == chunks - 1 and rows > 2:
-            out = out + border_copies(p, False, True)
+            out = out + border_copies(p, False, True) + edge_copies(p, False)
         return out
 
     def side_copies(p, c):
@@ -197,7 +220,7 @@
         return out
 
     def exchange(p, c):
-        return corner_copies(p, c) + side_copies(p, c)
+        return corner_copies(p, c) + side_copies(p, c) + ahead_copies(p, c)
 
     def start(jobs):
         for here, _, copies in jobs:
@@ -248,6 +271,47 @@
         new = mix(c, halo[s, pl.ds(y + 1, k)], halo[s, pl.ds(y - 1, k)], right, left,
                   fh[0, pl.ds(y, k)], fh[1, pl.ds(y, k)])
         return jnp.where(keep, new, 0.0)
+
+    ahead_column = jnp.logical_or(column == 1, column == PAD - 2)
+
+    def take_ahead(p, v, n):
+        def do(y, k, always=True):
+            got = ahead_column if always is True else jnp.logical_and(ahead_column, always)
+            new = jnp.where(got, landed[p, pl.ds(y, k)], new_halo(p * DEPTH, y, k))
+            halo[p * DEPTH + 1, pl.ds(y, k)] = jnp.where(keep, new, 0.0)
+        end = v + n
+        if v == 0:
+            v = 1
+            do(at(0, 1), 1, jnp.broadcast_to(jnp.logical_not(near_side(True)), column.shape))
+        if end == by and rows > 2:
+            end = by - 1
+            do(at(by - 1, 1), 1, jnp.broadcast_to(jnp.logical_not(near_side(False)), column.shape))
+        over(v, end - v, 16, do)
+
+    def send_ahead(p, c):
+        v, n = reach(p, c - 1), reach(p, c) - reach(p, c - 1)
+
+        def do(y, k):
+            for i, x in enumerate((pl.ds(0, PAD), pl.ds(bx - PAD, PAD))):
+                tile = main[p * DEPTH, pl.ds(y, k), x]
+                early[p, i, pl.ds(y, k)] = mix(
+                    tile, main[p * DEPTH, pl.ds(y + 1, k), x], main[p * DEPTH, pl.ds(y - 1, k), x],
+                    pltpu.roll(tile, PAD - 1, 1), pltpu.roll(tile, 1, 1),
+                    f[0, pl.ds(y, k), x], f[1, pl.ds(y, k), x])
+        end = v + n
+        if v == 0:
+            v = 1
+
+            @pl.when(jnp.logical_not(near_side(True)))
+            def _():
+                do(at(0, 1), 1)
+        if end == by and rows > 2:
+            end = by - 1
+
+            @pl.when(jnp.logical_not(near_side(False)))
+            def _():
+                do(at(by - 1, 1), 1)
+        over(v, end - v, 8, do)
 
     def over(v, n, k, do):
         if n <= 0:
@@ -274,6 +338,8 @@
         return do
 
     def advance(p, c):
+        cuts = plan[p]
+        chunks = len(cuts) - 1
         for i in range(1, DEPTH + 1):
             s = p * DEPTH + i
             ahead = STEPS - s
@@ -285,7 +351,10 @@
             if i < DEPTH:
                 low = low - 1 if c else 0
                 high = high if c == chunks - 1 else high - 1
-                over(low, high - low, 16, write_halo(s))
+                if i == 1:
+                    take_ahead(p, low, high - low)
+                else:
+                    over(low, high - low, 16, write_halo(s))
                 margin = DEPTH - i
                 for first in (True, False):
                     if c != (0 if first else chunks - 1) or not first and rows <= 2:
@@ -300,26 +369,33 @@
                             write_halo(s)(y, margin)
         return low, high
 
+    pieces = len(fine) - 1
+
     def share(c, to, sender):
-        n = cuts[c + 1] - cuts[c]
-        lines = pl.ds(pl.multiple_of(at(cuts[c], n) - top, 8), n)
+        if c < pieces:
+            n = fine[c + 1] - fine[c]
+            lines = pl.ds(pl.multiple_of(at(fine[c], n) - top, 8), n)
+        else:
+            lines = pl.ds(0, by)
         return pltpu.make_async_remote_copy(
             src_ref=stats.at[:, lines], dst_ref=gathered.at[sender, :, lines],
             send_sem=stat_send.at[c, to], recv_sem=stat_recv.at[c, sender],
             device_id={"cols": to}, device_id_type=MESH)
 
-    def each_peer(do):
-        if cols <= 8:
-            for k in range(cols):
+    def each_peer(low, high, do):
+        if high - low <= 8:
+            for k in range(low, high):
                 @pl.when(col != k)
                 def _():
                     do(k)
         else:
-            @pl.loop(0, cols)
+            @pl.loop(low, high)
             def _(k):
                 @pl.when(col != k)
                 def _():
                     do(k)
+
+    head = min(HEAD, cols) if pieces > 1 else 0
 
     def last_step(v, n):
         y = at(v, n)
@@ -338,8 +414,8 @@
             gathered[col, 1, out] = second
 
     def combine(c):
-        n = cuts[c + 1] - cuts[c]
-        y = at(cuts[c], n) - top
+        n = fine[c + 1] - fine[c]
+        y = at(fine[c], n) - top
 
         @pl.loop(0, n // 8)
         def _(i):
@@ -351,9 +427,22 @@
             moments[0, lines] = mean
             moments[1, lines] = lax.rsqrt(spread / (bx * cols) + 0.0001)
 
+    pl.semaphore_wait(barrier, across + upright)
     send_token(0)
+    for load in loads:
+        load.wait()
     for c in range(chunks):
         start(side_copies(0, c))
+        send_ahead(0, c)
+        start(ahead_copies(0, c))
+    @pl.loop(0, by // 4)
+    def _(i):
+        lines = pl.ds(i * 4, 4)
+        for d in range(2):
+            flow = f[d, pl.ds(top + i * 4, 4)]
+            weight[2 * d, lines] = 0.05 - flow
+            weight[2 * d + 1, lines] = 0.05 + flow
+
     known = 0
 
     def learn():
@@ -368,23 +457,61 @@
     while known < len(spread_to) - 1:
         known = learn()
     for p in range(PHASES):
-        for c in range(chunks):
-            finish(exchange(p, c))
+        taken = 0
+        for c in range(len(plan[p]) - 1):
+            while taken < chunks and cuts[taken] < plan[p][c + 1]:
+                finish(exchange(p, taken))
+                taken += 1
             low, high = advance(p, c)
             if p + 1 < PHASES:
-                start(exchange(p + 1, c))
+                start(side_copies(p + 1, c))
+                start(corner_copies(p + 1, c))
+                send_ahead(p + 1, c)
+                start(ahead_copies(p + 1, c))
             else:
                 last_step(low, high - low)
                 while known < len(spread_to):
                     known = learn()
-                each_peer(lambda k: share(c, k, col).start())
-    for c in range(chunks):
-        each_peer(lambda k: share(c, k, k).wait_recv())
-        combine(c)
+                if head:
+                    each_peer(0, head, lambda k: share(c, k, col).start())
+    def later(k):
+        @pl.when(k > col)
+        def _():
+            share(pieces, k, col).start()
+
+    def earlier(k):
+        @pl.when(k < col)
+        def _():
+            share(pieces, k, col).start()
+    each_peer(head, cols, later)
+
+    @pl.when(col > head)
+    def _():
+        pl.delay(HOLD)
+    each_peer(head, cols, earlier)
+    if head:
+        @pl.when(col < head)
+        def _():
+            for c in range(pieces):
+                each_peer(0, cols, lambda k: share(c, k, k).wait_recv())
+                combine(c)
+
+        @pl.when(col >= head)
+        def _():
+            each_peer(0, cols, lambda k: share(pieces, k, k).wait_recv())
+            for c in range(pieces):
+                combine(c)
+    else:
+        each_peer(0, cols, lambda k: share(pieces, k, k).wait_recv())
+        for c in range(pieces):
+            combine(c)
     for c in range(chunks):
         for p in range(PHASES):
             drain(exchange(p, c))
-        each_peer(lambda k: share(c, k, col).wait_send())
+    for c in range(pieces):
+        if head:
+            each_peer(0, head, lambda k: share(c, k, col).wait_send())
+    each_peer(head, cols, lambda k: share(pieces, k, col).wait_send())
 
 
 def scale_kernel(end, lines, scaled_out, end_out, scaled, sem):
@@ -406,14 +533,15 @@
 
 def shards(rows, cols, tracer, flow_y, flow_x):
     by, bx, species = tracer.shape
-    cuts = (0,) + tuple(cut for cut in CUTS if cut < by) + (by,)
+    cuts, fine = ((0,) + tuple(cut for cut in chosen if cut < by) + (by,) for chosen in (CUTS, FINE))
     chunks = len(cuts) - 1
+    pieces = len(fine) - 1
     tall = by + 2 * DEPTH
     block = jax.ShapeDtypeStruct(tracer.shape, jnp.float32)
     hbm = pl.BlockSpec(memory_space=pl.ANY)
     dma = pltpu.SemaphoreType.DMA
     end, lines = pl.pallas_call(
-        functools.partial(kernel, rows, cols, by, bx, cuts),
+        functools.partial(kernel, rows, cols, by, bx, cuts, fine),
         out_shape=(pltpu.VMEM(tracer.shape, jnp.float32), pltpu.VMEM((2, by, species), jnp.float32)),
         in_specs=[pl.BlockSpec(memory_space=pltpu.HBM)] * 3,
         out_specs=(pl.BlockSpec(memory_space=pltpu.VMEM),) * 2,
@@ -423,13 +551,16 @@
             pltpu.VMEM((2, tall, bx, species), jnp.float32),
             pltpu.VMEM((2, tall, PAD, species), jnp.float32),
             pltpu.VMEM((4, by, bx, species), jnp.float32),
+            pltpu.VMEM((PHASES, 2, tall, PAD, species), jnp.float32),
+            pltpu.VMEM((PHASES, tall, PAD, species), jnp.float32),
             pltpu.VMEM((2, by, species), jnp.float32),
             pltpu.VMEM((cols, 2, by, species), jnp.float32),
             dma((3,)),
-            dma((PHASES, chunks, 2, 2)), dma((PHASES, chunks, 2, 2)),
+            dma((PHASES, chunks, 2, 3)), dma((PHASES, chunks, 2, 3)),
             dma((PHASES, 2, 2)), dma((PHASES, 2, 2)),
             dma((PHASES, 2, 2, 2)), dma((PHASES, 2, 2, 2)),
-            dma((chunks, cols)), dma((chunks, cols)),
+            dma((PHASES, 2, 2, 2)), dma((PHASES, 2, 2, 2)),
+            dma((pieces + 1, cols)), dma((pieces + 1, cols)),
             pltpu.SemaphoreType.REGULAR((max(1, len(radii(cols))),)),
         ],
         compiler_params=pltpu.CompilerParams(

time: 25.6 us -> 24.6 us (0.961)
  Pallas kernels: 24.8 us -> 23.8 us
    pallas_call x1, Pallas kernels: 23.8 us -> 22.8 us  [shards(): pl.pallas_call(functools.partial(kernel, rows, cols, by, bx, cuts, fine),...]
where the time goes in v2:
time: 24.6 us; the launch traced here: 24.5 us
  Pallas kernels  23.8 us (97%)
  between operations  0.64 us (3%)
    pallas_call x1, Pallas kernels, shards(): pl.pallas_call(functools.partial(kernel, rows, cols, by, bx, cuts, fine),...  22.8 us
    pallas_call x1, Pallas kernels, shards(): pl.pallas_call(scale_kernel, out_shape=(block, block), in_specs=[pl.Block...  1.02 us

profile of v2, /device:TPU:0, one launch (start us, length us, event | category | flops | bytes accessed | tf_op | source)
XLA Modules:
  0.0 24.5 jit_solution(13475650943580288798)
XLA Ops:
  0.6 22.8 %shard_map.50 = (f32[32,32,128]{2,1,0:T(8,128)S(1)}, f32[2,32,128]{2,1,0:T(8,128)S(1)}) custom-call(f32[32,32,128]{2,1,0:T(8,128)} %t_hbm.1, f32[32,32,128]{2,1,0:T(8,128)} %fy_hbm.1, f32[32,32,128]{2,1,0:T(8,128)} %fx_hbm.1), custom_call_target="tpu_custom_call" | custom-call | tf_op jit(solution)/shard_map/pallas_call | solution.py:543
  23.4 1.0 %shard_map.51 = (f32[32,32,128]{2,1,0:T(8,128)}, f32[32,32,128]{2,1,0:T(8,128)}) custom-call(f32[32,32,128]{2,1,0:T(8,128)S(1)} %get-tuple-element.4.end, f32[2,32,128]{2,1,0:T(8,128)S(1)} %get-tuple-element.5.lines), custom_call_target="tpu_custom_call" | custom-call | tf_op jit(solution)/shard_map/pallas_call | solution.py:569

commit v3 on v2

--- a/solution.py
+++ b/solution.py
@@ -12,10 +12,10 @@
 PHASES = STEPS // DEPTH
 PAD = 8
 HALF = PAD // 2
-CUTS = (8,)
-FINE = (8,)
+CUTS = (16,)
+FINE = (16,)
 HEAD = 2
-HOLD = 1600
+HOLD = 2200
 SIDES = tuple((dy, dx) for dy in (-1, 1, 0) for dx in (-1, 1, 0) if (dy, dx) != (0, 0))
 CORNERS = tuple(side for side in SIDES if side[0] and side[1])
 
@@ -37,7 +37,7 @@
     tall = by + 2 * top
     chunks = len(cuts) - 1
     plan = [cuts] * (PHASES - 1) + [fine]
-    odd = lax.rem(row, 2) == 1
+    down = lax.rem(row, 2) == 0
 
     def exists(dy, dx):
         ok = None
@@ -48,7 +48,7 @@
         return ok
 
     def at(v, n):
-        return jnp.where(odd, top + v, top + by - v - n)
+        return jnp.where(down, top + v, top + by - v - n)
 
     barrier = pltpu.get_barrier_semaphore()
     for dy, dx in SIDES:
@@ -129,7 +129,7 @@
         return by if c == chunks - 1 else min(by, cuts[c + 1] + STEPS - 1 - p * DEPTH)
 
     def near_side(first):
-        return jnp.where(odd, row > 0, row < rows - 1) if first else jnp.where(odd, row < rows - 1, row > 0)
+        return jnp.where(down, row > 0, row < rows - 1) if first else jnp.where(down, row < rows - 1, row > 0)
 
     def column_copies(p, c):
         v, n = reach(p, c - 1), reach(p, c) - reach(p, c - 1)
@@ -179,8 +179,8 @@
     def border_copies(p, first, corners):
         out = []
         for i, dy in enumerate((-1, 1)):
-            here = odd if (dy < 0) == first else jnp.logical_not(odd)
-            there = odd if (dy > 0) == first else jnp.logical_not(odd)
+            here = down if (dy < 0) == first else jnp.logical_not(down)
+            there = down if (dy > 0) == first else jnp.logical_not(down)
             ys, yd = rows_of(dy, DEPTH)
             mine = [remote(main.at[p * DEPTH, ys], main.at[p * DEPTH, yd],
                            row_send.at[p, i, 0], row_recv.at[p, i, 0], dy, 0)]
@@ -205,17 +205,17 @@
 
     def corner_copies(p, c):
         out = []
-        if c == 0:
+        if c == 0 and rows > 2:
             out = border_copies(p, True, True) + edge_copies(p, True)
-        if c == chunks - 1 and rows > 2:
+        if c == chunks - 1:
             out = out + border_copies(p, False, True) + edge_copies(p, False)
         return out
 
     def side_copies(p, c):
         out = column_copies(p, c)
-        if c == 0:
+        if c == 0 and rows > 2:
             out = out + border_copies(p, True, False)
-        if c == chunks - 1 and rows > 2:
+        if c == chunks - 1:
             out = out + border_copies(p, False, False)
         return out
 
@@ -280,10 +280,10 @@
             new = jnp.where(got, landed[p, pl.ds(y, k)], new_halo(p * DEPTH, y, k))
             halo[p * DEPTH + 1, pl.ds(y, k)] = jnp.where(keep, new, 0.0)
         end = v + n
-        if v == 0:
+        if v == 0 and rows > 2:
             v = 1
             do(at(0, 1), 1, jnp.broadcast_to(jnp.logical_not(near_side(True)), column.shape))
-        if end == by and rows > 2:
+        if end == by:
             end = by - 1
             do(at(by - 1, 1), 1, jnp.broadcast_to(jnp.logical_not(near_side(False)), column.shape))
         over(v, end - v, 16, do)
@@ -299,13 +299,13 @@
                     pltpu.roll(tile, PAD - 1, 1), pltpu.roll(tile, 1, 1),
                     f[0, pl.ds(y, k), x], f[1, pl.ds(y, k), x])
         end = v + n
-        if v == 0:
+        if v == 0 and rows > 2:
             v = 1
 
             @pl.when(jnp.logical_not(near_side(True)))
             def _():
                 do(at(0, 1), 1)
-        if end == by and rows > 2:
+        if end == by:
             end = by - 1
 
             @pl.when(jnp.logical_not(near_side(False)))
@@ -357,10 +357,10 @@
                     over(low, high - low, 16, write_halo(s))
                 margin = DEPTH - i
                 for first in (True, False):
-                    if c != (0 if first else chunks - 1) or not first and rows <= 2:
+                    if c != (0 if first else chunks - 1) or first and rows <= 2:
                         continue
                     for dy in (-1, 1):
-                        here = odd if (dy < 0) == first else jnp.logical_not(odd)
+                        here = down if (dy < 0) == first else jnp.logical_not(down)
 
                         @pl.when(jnp.logical_and(here, exists(dy, 0)))
                         def _():

time: 24.6 us -> 23.8 us (0.967)
  Pallas kernels: 23.8 us -> 23 us
    pallas_call x1, Pallas kernels: 22.8 us -> 22 us  [shards(): pl.pallas_call(functools.partial(kernel, rows, cols, by, bx, cuts, fine),...]
where the time goes in v3:
time: 23.8 us; the launch traced here: 23.6 us
  Pallas kernels  23 us (97%)
  between operations  0.64 us (3%)
    pallas_call x1, Pallas kernels, shards(): pl.pallas_call(functools.partial(kernel, rows, cols, by, bx, cuts, fine),...  22 us
    pallas_call x1, Pallas kernels, shards(): pl.pallas_call(scale_kernel, out_shape=(block, block), in_specs=[pl.Block...  1.02 us

profile of v3, /device:TPU:0, one launch (start us, length us, event | category | flops | bytes accessed | tf_op | source)
XLA Modules:
  0.0 23.6 jit_solution(7450516627021466425)
XLA Ops:
  0.6 22.0 %shard_map.50 = (f32[32,32,128]{2,1,0:T(8,128)S(1)}, f32[2,32,128]{2,1,0:T(8,128)S(1)}) custom-call(f32[32,32,128]{2,1,0:T(8,128)} %t_hbm.1, f32[32,32,128]{2,1,0:T(8,128)} %fy_hbm.1, f32[32,32,128]{2,1,0:T(8,128)} %fx_hbm.1), custom_call_target="tpu_custom_call" | custom-call | tf_op jit(solution)/shard_map/pallas_call | solution.py:543
  22.6 1.0 %shard_map.51 = (f32[32,32,128]{2,1,0:T(8,128)}, f32[32,32,128]{2,1,0:T(8,128)}) custom-call(f32[32,32,128]{2,1,0:T(8,128)S(1)} %get-tuple-element.4.end, f32[2,32,128]{2,1,0:T(8,128)S(1)} %get-tuple-element.5.lines), custom_call_target="tpu_custom_call" | custom-call | tf_op jit(solution)/shard_map/pallas_call | solution.py:569

commit v4 on v3

--- a/solution.py
+++ b/solution.py
@@ -15,7 +15,7 @@
 CUTS = (16,)
 FINE = (16,)
 HEAD = 2
-HOLD = 2200
+HOLD = (1500, 2500)
 SIDES = tuple((dy, dx) for dy in (-1, 1, 0) for dx in (-1, 1, 0) if (dy, dx) != (0, 0))
 CORNERS = tuple(side for side in SIDES if side[0] and side[1])
 
@@ -31,7 +31,7 @@
 def kernel(rows, cols, by, bx, cuts, fine, t_hbm, fy_hbm, fx_hbm, final, moments,
            main, halo, f, fh, weight, early, landed, stats, gathered,
            load_sem, col_send, col_recv, row_send, row_recv, corner_send, corner_recv,
-           edge_send, edge_recv,           stat_send, stat_recv, tokens):
+           edge_send, edge_recv,           stat_send, stat_recv, tokens, heard):
     row, col = lax.axis_index("rows"), lax.axis_index("cols")
     top = DEPTH
     tall = by + 2 * top
@@ -332,6 +332,39 @@
             main[s, pl.ds(y, k)] = new_main(s - 1, y, k, beyond)
         return do
 
+    def write_edges(s):
+        def do(y, k):
+            lines = pl.ds(y, k)
+            for x, wide in (
+                (0, (halo[s - 1, lines], main[s - 1, lines, pl.ds(0, 2 * PAD)])),
+                (bx - PAD, (main[s - 1, lines, pl.ds(bx - 2 * PAD, 2 * PAD)], halo[s - 1, lines])),
+            ):
+                tile = pl.ds(x, PAD)
+                wide = jnp.concatenate(wide, axis=1)
+                right = pltpu.roll(wide, 3 * PAD - 1, 1)[:, PAD:2 * PAD]
+                left = pltpu.roll(wide, 1, 1)[:, PAD:2 * PAD]
+                up, down, front, back = (weight[i, pl.ds(y - top, k), tile] for i in range(4))
+                main[s, lines, tile] = (
+                    (0.8 * wide[:, PAD:2 * PAD] + up * main[s - 1, pl.ds(y + 1, k), tile])
+                    + down * main[s - 1, pl.ds(y - 1, k), tile]
+                ) + (front * right + back * left)
+        return do
+
+    def settle(p):
+        def step(s):
+            def do(y, k):
+                c = main[s - 1, pl.ds(y, k)]
+                up, down, front, back = (weight[i, pl.ds(y - top, k)] for i in range(4))
+                main[s, pl.ds(y, k)] = (
+                    (0.8 * c + up * main[s - 1, pl.ds(y + 1, k)]) + down * main[s - 1, pl.ds(y - 1, k)]
+                ) + (front * pltpu.roll(c, bx - 1, 1) + back * pltpu.roll(c, 1, 1))
+            return do
+        for i in range(1, DEPTH + 1):
+            s = p * DEPTH + i
+            if s < STEPS:
+                low = i if rows > 2 else 0
+                over(low, by - i - low, 8, step(s))
+
     def write_halo(s):
         def do(y, k):
             halo[s, pl.ds(y, k)] = new_halo(s - 1, y, k)
@@ -347,7 +380,11 @@
             high = by if c == chunks - 1 else min(by, cuts[c + 1] + ahead)
             if s == STEPS:
                 break
-            over(low, high - low, 8, write_main(s))
+            start_v = max(low, DEPTH if rows > 2 else 0)
+            end_v = min(high, by - DEPTH)
+            over(low, start_v - low, 8, write_main(s))
+            over(start_v, end_v - start_v, 8, write_edges(s))
+            over(end_v, high - end_v, 8, write_main(s))
             if i < DEPTH:
                 low = low - 1 if c else 0
                 high = high if c == chunks - 1 else high - 1
@@ -428,6 +465,10 @@
             moments[1, lines] = lax.rsqrt(spread / (bx * cols) + 0.0001)
 
     pl.semaphore_wait(barrier, across + upright)
+    for dy in (-1, 1):
+        @pl.when(exists(dy, 0))
+        def _():
+            pl.semaphore_signal(heard, inc=1, device_id={"rows": row + dy}, device_id_type=MESH)
     send_token(0)
     for load in loads:
         load.wait()
@@ -450,22 +491,22 @@
         send_token(known + 1)
         return known + 1
 
-    if spread_to:
-        known = learn()
+    pl.semaphore_wait(heard, upright)
     for c in range(chunks):
         start(corner_copies(0, c))
     while known < len(spread_to) - 1:
         known = learn()
     for p in range(PHASES):
         taken = 0
+        settle(p)
         for c in range(len(plan[p]) - 1):
             while taken < chunks and cuts[taken] < plan[p][c + 1]:
                 finish(exchange(p, taken))
                 taken += 1
             low, high = advance(p, c)
             if p + 1 < PHASES:
+                start(corner_copies(p + 1, c))
                 start(side_copies(p + 1, c))
-                start(corner_copies(p + 1, c))
                 send_ahead(p + 1, c)
                 start(ahead_copies(p + 1, c))
             else:
@@ -485,9 +526,13 @@
             share(pieces, k, col).start()
     each_peer(head, cols, later)
 
-    @pl.when(col > head)
+    @pl.when(jnp.logical_and(col > head, col < cols - 2))
     def _():
-        pl.delay(HOLD)
+        pl.delay(HOLD[0])
+
+    @pl.when(jnp.logical_and(col > head, col >= cols - 2))
+    def _():
+        pl.delay(HOLD[1])
     each_peer(head, cols, earlier)
     if head:
         @pl.when(col < head)
@@ -562,6 +607,7 @@
             dma((PHASES, 2, 2, 2)), dma((PHASES, 2, 2, 2)),
             dma((pieces + 1, cols)), dma((pieces + 1, cols)),
             pltpu.SemaphoreType.REGULAR((max(1, len(radii(cols))),)),
+            pltpu.SemaphoreType.REGULAR,
         ],
         compiler_params=pltpu.CompilerParams(
             collective_id=0, has_side_effects=True, vmem_limit_bytes=67043328 - 1024 * 1024),

time: 23.8 us -> 23.8 us (level)
  no operation moved by 1% of the time
where the time goes in v4:
time: 23.8 us; the launch traced here: 23.6 us
  Pallas kernels  23 us (97%)
  between operations  0.64 us (3%)
    pallas_call x1, Pallas kernels, shards(): pl.pallas_call(functools.partial(kernel, rows, cols, by, bx, cuts, fine),...  21.9 us
    pallas_call x1, Pallas kernels, shards(): pl.pallas_call(scale_kernel, out_shape=(block, block), in_specs=[pl.Block...  1.02 us

profile of v4, /device:TPU:0, one launch (start us, length us, event | category | flops | bytes accessed | tf_op | source)
XLA Modules:
  0.0 23.6 jit_solution(15779677027185106844)
XLA Ops:
  0.6 21.9 %shard_map.50 = (f32[32,32,128]{2,1,0:T(8,128)S(1)}, f32[2,32,128]{2,1,0:T(8,128)S(1)}) custom-call(f32[32,32,128]{2,1,0:T(8,128)} %t_hbm.1, f32[32,32,128]{2,1,0:T(8,128)} %fy_hbm.1, f32[32,32,128]{2,1,0:T(8,128)} %fx_hbm.1), custom_call_target="tpu_custom_call" | custom-call | tf_op jit(solution)/shard_map/pallas_call | solution.py:588
  22.6 1.0 %shard_map.51 = (f32[32,32,128]{2,1,0:T(8,128)}, f32[32,32,128]{2,1,0:T(8,128)}) custom-call(f32[32,32,128]{2,1,0:T(8,128)S(1)} %get-tuple-element.4.end, f32[2,32,128]{2,1,0:T(8,128)S(1)} %get-tuple-element.5.lines), custom_call_target="tpu_custom_call" | custom-call | tf_op jit(solution)/shard_map/pallas_call | solution.py:615

commit v5 on v4

--- a/solution.py
+++ b/solution.py
@@ -13,7 +13,7 @@
 PAD = 8
 HALF = PAD // 2
 CUTS = (16,)
-FINE = (16,)
+FINE = (16, 24)
 HEAD = 2
 HOLD = (1500, 2500)
 SIDES = tuple((dy, dx) for dy in (-1, 1, 0) for dx in (-1, 1, 0) if (dy, dx) != (0, 0))

time: 23.8 us -> 23.7 us (level)
  no operation moved by 1% of the time
where the time goes in v5:
time: 23.7 us; the launch traced here: 23.6 us
  Pallas kernels  23 us (97%)
  between operations  0.64 us (3%)
    pallas_call x1, Pallas kernels, shards(): pl.pallas_call(functools.partial(kernel, rows, cols, by, bx, cuts, fine),...  21.9 us
    pallas_call x1, Pallas kernels, shards(): pl.pallas_call(scale_kernel, out_shape=(block, block), in_specs=[pl.Block...  1.02 us

profile of v5, /device:TPU:0, one launch (start us, length us, event | category | flops | bytes accessed | tf_op | source)
XLA Modules:
  0.0 23.6 jit_solution(17321980803615044788)
XLA Ops:
  0.6 21.9 %shard_map.50 = (f32[32,32,128]{2,1,0:T(8,128)S(1)}, f32[2,32,128]{2,1,0:T(8,128)S(1)}) custom-call(f32[32,32,128]{2,1,0:T(8,128)} %t_hbm.1, f32[32,32,128]{2,1,0:T(8,128)} %fy_hbm.1, f32[32,32,128]{2,1,0:T(8,128)} %fx_hbm.1), custom_call_target="tpu_custom_call" | custom-call | tf_op jit(solution)/shard_map/pallas_call | solution.py:588
  22.6 1.0 %shard_map.51 = (f32[32,32,128]{2,1,0:T(8,128)}, f32[32,32,128]{2,1,0:T(8,128)}) custom-call(f32[32,32,128]{2,1,0:T(8,128)S(1)} %get-tuple-element.4.end, f32[2,32,128]{2,1,0:T(8,128)S(1)} %get-tuple-element.5.lines), custom_call_target="tpu_custom_call" | custom-call | tf_op jit(solution)/shard_map/pallas_call | solution.py:615
